TPU v7x, 128 devices: a whole 4x4x4 slice. The times are simulated.
128 devices in a mesh: mx: 4 (over z), my: 4 (over y_hi, core), col: 8 (over y_lo, x).
Axes of the slice: x: 4, y: 4 (y_hi: 2, y_lo: 2; y = y_hi * 2 + y_lo), z: 4, core: 2. Of those that a mesh axis runs over, the one named last changes fastest.
Arguments:
- spectrum: float32 [2, 16, 128, 32, 512], P(None, 'col', None, 'mx', 'my'), may hold values from -6 to 6
- core_tensor: float32 [2, 64, 64, 16, 16, 16], P(None, 'col', None, ('mx', 'my')), may hold values from -0.01171875 to 0.01171875
- input_factor: float32 [128, 64], replicated, may hold values from -0.5 to 0.5
- output_factor: float32 [128, 64], replicated, may hold values from -0.75 to 0.75
- first_factor: float32 [32, 16], P('mx'), may hold values from -5 to 5
- second_factor: float32 [32, 16], P('my'), may hold values from -5 to 5
- third_factor: float32 [16, 16], replicated, may hold values from -5 to 5
Outputs:
- mixed_modes: float32 [2, 16, 128, 32, 512], P(None, 'col', None, 'mx', 'my')
All inputs are finite; a program needn't handle non-finite values.
Results may differ from a plain program's by a relative error of at most 0.00007.
Values sent between devices are 32-bit elements; how exact they have to be, the bound alone decides.
No kernel may reach another device: no remote copies, remote signals or barrier semaphores. Data moves between devices by JAX's collectives and lax.ppermute only.
A program may use at most 128 MiB of HBM per device.

v0:
```python
import jax
import jax.numpy as jnp
from jax import lax
from jax.sharding import PartitionSpec as P

precise = lax.Precision.HIGHEST


def per_device(
    spectrum, core_tensor, input_factor, output_factor, first_factor, second_factor, third_factor
):
    rank_local = core_tensor.shape[1]
    rank_out = core_tensor.shape[2]
    rows_first = first_factor.shape[0]
    rank_second = second_factor.shape[1]
    modes_third = third_factor.shape[0]
    core_third = jnp.einsum("cpqstu,zu->cpqstz", core_tensor, third_factor, precision=precise)
    core_third = core_third.reshape(
        2, rank_local, rank_out, core_tensor.shape[3], rank_second * modes_third
    )
    core_gathered = lax.all_gather(core_third, ("mx", "my"), axis=3, tiled=True)
    weight_first = jnp.einsum("cpqsm,ks->cpqkm", core_gathered, first_factor, precision=precise)
    weight_first = weight_first.reshape(
        2, rank_local, rank_out, rows_first, rank_second, modes_third
    )
    mode_weight = jnp.einsum("cpqktz,yt->cpqkyz", weight_first, second_factor, precision=precise)
    mode_weight = mode_weight.reshape(2, rank_local, rank_out, rows_first, -1)
    projected = jnp.einsum("cbikm,ir->cbrkm", spectrum, input_factor, precision=precise)
    rank_spectrum = lax.all_to_all(projected, "col", split_axis=2, concat_axis=1, tiled=True)
    real_part = jnp.einsum(
        "brkm,rqkm->bqkm", rank_spectrum[0], mode_weight[0], precision=precise
    ) - jnp.einsum("brkm,rqkm->bqkm", rank_spectrum[1], mode_weight[1], precision=precise)
    imag_part = jnp.einsum(
        "brkm,rqkm->bqkm", rank_spectrum[0], mode_weight[1], precision=precise
    ) + jnp.einsum("brkm,rqkm->bqkm", rank_spectrum[1], mode_weight[0], precision=precise)
    mode_values = jnp.stack([real_part, imag_part])
    summed_values = lax.psum_scatter(mode_values, "col", scatter_dimension=1, tiled=True)
    mixed_modes = jnp.einsum("oq,cbqkm->cbokm", output_factor, summed_values, precision=precise)
    return mixed_modes


def solution(mesh):
    placed = (
        P(None, "col", None, "mx", "my"),
        P(None, "col", None, ("mx", "my"), None, None),
        P(),
        P(),
        P("mx", None),
        P("my", None),
        P(),
    )
    return jax.shard_map(
        per_device,
        mesh=mesh,
        in_specs=placed,
        out_specs=P(None, "col", None, "mx", "my"),
        check_vma=False,
    )
```

profile of v0, /device:TPU:1, one launch (start us, length us, event | category | flops | bytes accessed | tf_op | source)
XLA Modules:
  0.0 377.2 jit_solution(9555578541024835973)
XLA Ops:
  6.5 0.0 copy-start
  6.5 0.0 copy-start.4
  6.5 0.0 all-gather.2.cloned.1.call-start
  6.5 1.6 copy-done
  8.1 3.9 %fusion.22 = f32[2,8,64,16,16]{2,4,3,1,0:T(8,128)} fusion(f32[2,8,64,1,16,16]{2,5,4,3,1,0:T(8,128)S(1)} %copy-done, f32[16,16]{1,0:T(8,128)} %param.13), kind=kOutput, calls=%fused_computation.17 | convolution fusion | flops 50331648 | bytes 2098176 | tf_op jit(solution)/shard_map/cpqstu,zu->cpqstz/dot_general | solution.py:17
  12.1 3.2 copy.51
  15.2 0.0 all-gather.2.cloned.1.call-update
  15.2 0.0 reduce-scatter.2.cloned.1.call-start
  15.3 0.0 copy-done.4
  15.3 3.1 fusion.26
  18.4 0.6 copy.57
  19.0 20.6 %all_to_all.15 = f32[2,2,64,8,128]{4,3,1,0,2:T(8,128)S(1)} all-to-all(f32[2,2,64,8,128]{4,3,1,0,2:T(8,128)S(1)} %copy.57), channel_id=1, replica_groups=mesh['mx'=4,'my'=4,'col'=8] {'col'}, dimensions={2} | all-to-all | bytes 2097152 | tf_op jit(solution)/shard_map/all_to_all | solution.py:29
  39.6 0.1 copy.58
  39.7 0.1 fusion.36
  39.9 0.0 copy-start.6
  39.9 3.2 copy.61
  43.1 3.1 copy.65
  46.2 90.1 %all-gather.2.cloned.1.call-done = f32[2,8,64,16,256]{4,2,1,0,3:T(8,128)} async-done(((f32[2,8,64,1,256]{4,2,1,0,3:T(8,128)}), f32[2,8,64,16,256]{4,2,1,0,3:T(8,128)}) %all-gather.2.cloned.1.call-update) | async-done | bytes 16777232 | tf_op jit(solution)/shard_map/all_gather | solution.py:21
  136.3 0.0 copy-done.6
  136.3 25.8 %fusion.16 = f32[2,8,64,8,256]{4,3,2,1,0:T(8,128)} fusion(f32[2,8,64,16,256]{4,2,1,0,3:T(8,128)} %all-gather.2.cloned.1.call-done, f32[8,16]{1,0:T(8,128)S(1)} %copy-done.6), kind=kOutput, calls=%fused_computation.15 | convolution fusion | flops 402653184 | bytes 25166336 | tf_op jit(solution)/shard_map/cpqsm,ks->cpqkm/dot_general | solution.py:22
  162.1 0.0 copy-start.7
  162.1 12.2 %copy.53 = f32[2,8,64,8,256]{2,4,3,1,0:T(8,128)} copy(f32[2,8,64,8,256]{4,3,2,1,0:T(8,128)} %fusion.16) | data formatting | bytes 16777216 | tf_op jit(solution)/shard_map/cpqsm,ks->cpqkm/transpose | solution.py:22
  174.3 0.0 copy-done.7
  174.4 17.9 %fusion.19 = f32[2,8,64,8,8,16]{2,4,5,3,1,0:T(8,128)S(1)} fusion(f32[2,8,64,8,16,16]{2,5,4,3,1,0:T(8,128)} %bitcast.59, f32[8,16]{1,0:T(8,128)S(1)} %copy-done.7), kind=kOutput, calls=%fused_computation.16 | convolution fusion | flops 201326592 | bytes 12583424 | tf_op jit(solution)/shard_map/cpqktz,yt->cpqkyz/dot_general | solution.py:26
  192.2 1.1 fusion.35
  193.3 0.9 copy.55
  194.2 0.0 copy-start.2
  194.2 0.9 copy.62
  195.2 1.2 copy-done.2
  196.4 0.0 copy-start.3
  196.4 14.4 %fusion.4 = f32[8,128,64,16]{2,3,1,0:T(8,128)S(1)} fusion(f32[16,8,8,128]{0,1,3,2:T(8,128)S(1)} %copy-done.2, f32[8,64,8,128]{1,3,2,0:T(8,128)S(1)} %bitcast.60), kind=kOutput, calls=%fused_computation.7 | convolution fusion | flops 100663296 | bytes 6815744 | tf_op jit(solution)/shard_map/brkm,rqkm->bqkm/dot_general | solution.py:33
  210.8 0.0 copy-done.3
  210.8 14.6 %fusion.6 = f32[8,128,64,16]{2,3,1,0:T(8,128)S(1)} fusion(f32[16,8,8,128]{0,1,3,2:T(8,128)S(1)} %copy-done.3, f32[8,64,8,128]{1,3,2,0:T(8,128)S(1)} %bitcast.61), kind=kOutput, calls=%fused_computation.9 | convolution fusion | flops 100663296 | bytes 6815744 | tf_op jit(solution)/shard_map/brkm,rqkm->bqkm/dot_general | solution.py:32
  225.4 14.3 %add_bitcast_fusion = f32[1,16,64,8,128]{2,1,4,3,0:T(8,128)S(1)} fusion(f32[8,128,64,16]{2,3,1,0:T(8,128)S(1)} %fusion.4, f32[16,8,8,128]{0,1,3,2:T(8,128)S(1)} %copy-done.3, f32[8,64,8,128]{1,3,2,0:T(8,128)S(1)} %bitcast.57), kind=kOutput, calls=%fused_computation.5 | convolution fusion | flops 101711872 | bytes 11010048 | tf_op jit(solution)/shard_map/brkm,rqkm->bqkm/dot_general | solution.py:35
  239.8 14.4 %subtract_bitcast_fusion = f32[1,16,64,8,128]{2,1,4,3,0:T(8,128)S(1)} fusion(f32[8,128,64,16]{2,3,1,0:T(8,128)S(1)} %fusion.6, f32[16,8,8,128]{0,1,3,2:T(8,128)S(1)} %copy-done.2, f32[8,64,8,128]{1,3,2,0:T(8,128)S(1)} %bitcast.58), kind=kOutput, calls=%fused_computation.6 | convolution fusion | flops 101711872 | bytes 11010048 | tf_op jit(solution)/shard_map/brkm,rqkm->bqkm/dot_general | solution.py:30
  254.2 6.1 %pad_maximum_fusion = f32[2,16,64,8,128]{2,1,4,3,0:T(8,128)} fusion(f32[1,16,64,8,128]{2,1,4,3,0:T(8,128)S(1)} %add_bitcast_fusion, f32[1,16,64,8,128]{2,1,4,3,0:T(8,128)S(1)} %subtract_bitcast_fusion), kind=kLoop, calls=%fused_computation | loop fusion | flops 2097152 | bytes 16777216 | tf_op jit(solution)/shard_map/stack | solution.py:36
  260.3 11.0 %copy.70 = f32[2,16,64,8,128]{4,3,2,0,1:T(8,128)} copy(f32[2,16,64,8,128]{2,1,4,3,0:T(8,128)} %pad_maximum_fusion) | data formatting | bytes 16777216 | tf_op jit(solution)/shard_map/stack | solution.py:36
  271.3 0.0 copy-start.5
  271.3 0.0 reduce-scatter.2.cloned.1.call-update
  271.3 0.0 copy-start.1
  271.3 89.9 %reduce-scatter.2.cloned.1.call-done = f32[2,2,64,8,128]{4,3,2,0,1:T(8,128)} async-done(((f32[2,16,64,8,128]{4,3,2,0,1:T(8,128)}), f32[2,2,64,8,128]{4,3,2,0,1:T(8,128)}) %reduce-scatter.2.cloned.1.call-update) | async-done | bytes 1048592 | tf_op jit(solution)/shard_map/reduce_scatter | solution.py:37
  361.2 0.0 copy-done.5
  361.2 6.0 %convolution_bitcast_fusion = f32[2,2,128,8,128]{2,4,3,1,0:T(8,128)} fusion(f32[2,2,64,8,128]{4,3,2,0,1:T(8,128)} %reduce-scatter.2.cloned.1.call-done, f32[128,64]{0,1:T(8,128)S(1)} %copy-done.5), kind=kOutput, calls=%fused_computation.21 | convolution fusion | flops 402653184 | bytes 3178496 | tf_op jit(solution)/shard_map/oq,cbqkm->cbokm/dot_general | solution.py:38
  367.2 2.9 copy.72
  370.1 0.0 copy-done.1
  (2 shorter events, 0.1 us)
Async XLA Ops:
  6.5 1.6 copy-start
  6.5 8.8 %copy-start.4 = (f32[128,64]{0,1:T(8,128)S(1)}, f32[128,64]{0,1:T(8,128)}, u32[]{:S(2)}) copy-start(f32[128,64]{0,1:T(8,128)} %param.9) | copy-start | bytes 98308
  6.5 129.7 %all-gather.2.cloned.1.call-start = ((), (), s32[]{:S(2)}) async-start(), calls=%async_computation.2 | async-start | bytes 17825792 | tf_op jit(solution)/shard_map/all_gather | solution.py:21
  15.2 346.0 %reduce-scatter.2.cloned.1.call-start = ((), (), s32[]{:S(2)}) async-start(), calls=%async_computation.3 | async-start | bytes 9437184 | tf_op jit(solution)/shard_map/reduce_scatter | solution.py:37
  39.9 96.3 %copy-start.6 = (f32[8,16]{1,0:T(8,128)S(1)}, f32[8,16]{1,0:T(8,128)}, u32[]{:S(2)}) copy-start(f32[8,16]{1,0:T(8,128)} %param.11) | copy-start | bytes 1540
  162.1 12.2 %copy-start.7 = (f32[8,16]{1,0:T(8,128)S(1)}, f32[8,16]{1,0:T(8,128)}, u32[]{:S(2)}) copy-start(f32[8,16]{1,0:T(8,128)} %param.12) | copy-start | bytes 1540
  194.2 2.2 copy-start.2
  196.4 14.4 %copy-start.3 = (f32[16,8,8,128]{0,1,3,2:T(8,128)S(1)}, f32[16,8,8,128]{0,1,3,2:T(8,128)}, u32[]{:S(2)}) copy-start(f32[16,8,8,128]{0,1,3,2:T(8,128)} %copy.65) | copy-start | bytes 1572868
  271.3 89.9 %copy-start.5 = (f32[128,64]{0,1:T(8,128)S(1)}, f32[128,64]{0,1:T(8,128)}, u32[]{:S(2)}) copy-start(f32[128,64]{0,1:T(8,128)} %param.10) | copy-start | bytes 98308
  271.3 98.8 %copy-start.1 = (f32[2,8,64,1,16,16]{2,5,4,3,1,0:T(8,128)S(1)}, f32[2,8,64,1,16,16]{2,5,4,3,1,0:T(8,128)}, u32[]{:S(2)}) copy-start(f32[2,8,64,1,16,16]{2,5,4,3,1,0:T(8,128)} %param.8) | copy-start | bytes 3145732
Sparse Core Ops, SparseCore 0:
  15.4 120.8 all-gather.1
  271.4 89.7 reduce-scatter.1
where the time goes:
time: 383 us; the launch traced here: 377 us
  waiting for transfers between devices  180 us (47%)
  matrix products  114 us (30%)
  local copies, waits for them, and re-layouts  42.2 us (11%)
  blocking collectives  20.6 us (5%)
  between operations  13.8 us (4%)
  other arithmetic  6.1 us (2%)
    all_gather x1, waiting for transfers between devices, per_device(): core_gathered = lax.all_gather(core_third, ('mx', 'my'), axis=3, tiled=True)  90.1 us
    reduce_scatter x1, waiting for transfers between devices, per_device(): lax.psum_scatter(mode_values, 'col', scatter_dimension=1, tiled=True)  89.9 us
    dot_general x1, matrix products, per_device(): jnp.einsum('cpqsm,ks->cpqkm', core_gathered, first_factor, precision=prec...  25.8 us
    all_to_all x1, blocking collectives, per_device(): lax.all_to_all(projected, 'col', split_axis=2, concat_axis=1, tiled=True)  20.6 us
    dot_general x1, matrix products, per_device(): jnp.einsum('cpqktz,yt->cpqkyz', weight_first, second_factor, precision=pr...  17.9 us
    dot_general x1, matrix products, per_device(): jnp.einsum('brkm,rqkm->bqkm', rank_spectrum[1], mode_weight[1], precision...  14.6 us
    dot_general x1, matrix products, per_device(): jnp.einsum('brkm,rqkm->bqkm', rank_spectrum[0], mode_weight[1], precision...  14.4 us
    dot_general x1, matrix products, per_device(): jnp.einsum('brkm,rqkm->bqkm', rank_spectrum[0], mode_weight[0], precision...  14.4 us
  transfers between devices with their start and end apart: 2, of which 2 were waited for; matrix products, arithmetic and copies ran while one was open for 3% of the time, Pallas kernels for 0%

commit v1 on v0

--- a/solution.py
+++ b/solution.py
@@ -4,6 +4,13 @@
 from jax.sharding import PartitionSpec as P
 
 precise = lax.Precision.HIGHEST
+
+
+def swapped_in(x, mesh_axis, d):
+    n_dev = lax.axis_size(mesh_axis)
+    blocks = jnp.stack([x for _ in range(n_dev)])
+    blocks = lax.all_to_all(blocks, mesh_axis, split_axis=0, concat_axis=0)
+    return jnp.concatenate(blocks, axis=d)
 
 
 def per_device(
@@ -18,7 +25,7 @@
     core_third = core_third.reshape(
         2, rank_local, rank_out, core_tensor.shape[3], rank_second * modes_third
     )
-    core_gathered = lax.all_gather(core_third, ("mx", "my"), axis=3, tiled=True)
+    core_gathered = swapped_in(core_third, ("mx", "my"), 3)
     weight_first = jnp.einsum("cpqsm,ks->cpqkm", core_gathered, first_factor, precision=precise)
     weight_first = weight_first.reshape(
         2, rank_local, rank_out, rows_first, rank_second, modes_third

time: 383 us -> 485 us (1.27)
  waiting for transfers between devices: 180 us -> 278 us
  blocking collectives: 20.6 us -> 0 us
  starting transfers between devices: 0.04 us -> 14.3 us
  local copies, waits for them, and re-layouts: 42.2 us -> 49.9 us
    all_to_all x0 -> x2, waiting for transfers between devices: none -> 190 us  [the longest x1 178 us: swapped_in(): blocks = lax.all_to_all(blocks, mesh_axis, split_axis=0, concat_axis=0)]
    all_gather x1 -> x0, waiting for transfers between devices: 90.1 us -> none  [per_device(): core_gathered = lax.all_gather(core_third, ('mx', 'my'), axis=3, tiled=True)]
    all_to_all x1 -> x0, blocking collectives: 20.6 us -> none  [per_device(): lax.all_to_all(projected, 'col', split_axis=2, concat_axis=1, tiled=True)]
    all_to_all x0 -> x2, starting transfers between devices: none -> 14.3 us  [the longest x1 8.45 us: swapped_in(): blocks = lax.all_to_all(blocks, mesh_axis, split_axis=0, concat_axis=0)]
    another operation x0 -> x2, local copies, waits for them, and re-layouts: none -> 8.44 us  [swapped_in(): blocks = jnp.stack([x for _ in range(n_dev)])]
  transfers between devices with their start and end apart: 2 -> 3, of which waited for: 2 -> 3; matrix products, arithmetic and copies ran while one was open for 3% -> 3% of each run, Pallas kernels for 0% -> 0%
where the time goes in v1:
time: 485 us; the launch traced here: 478 us
  waiting for transfers between devices  278 us (57%)
  matrix products  115 us (24%)
  local copies, waits for them, and re-layouts  49.9 us (10%)
  starting transfers between devices  14.3 us (3%)
  between operations  14.1 us (3%)
  other arithmetic  6.12 us (1%)
    all_to_all x1, waiting for transfers between devices, swapped_in(): blocks = lax.all_to_all(blocks, mesh_axis, split_axis=0, concat_axis=0)  178 us
    reduce_scatter x1, waiting for transfers between devices, per_device(): lax.psum_scatter(mode_values, 'col', scatter_dimension=1, tiled=True)  88.4 us
    dot_general x1, matrix products, per_device(): jnp.einsum('cpqsm,ks->cpqkm', core_gathered, first_factor, precision=prec...  25.9 us
    dot_general x1, matrix products, per_device(): jnp.einsum('cpqktz,yt->cpqkyz', weight_first, second_factor, precision=pr...  17.9 us
    dot_general x1, matrix products, per_device(): jnp.einsum('brkm,rqkm->bqkm', rank_spectrum[0], mode_weight[0], precision...  16.3 us
    dot_general x1, matrix products, per_device(): jnp.einsum('brkm,rqkm->bqkm', rank_spectrum[1], mode_weight[1], precision...  14.6 us
    dot_general x1, matrix products, per_device(): jnp.einsum('brkm,rqkm->bqkm', rank_spectrum[1], mode_weight[0], precision...  14.4 us
    dot_general x1, matrix products, per_device(): jnp.einsum('brkm,rqkm->bqkm', rank_spectrum[0], mode_weight[1], precision...  14.3 us
  transfers between devices with their start and end apart: 3, of which 3 were waited for; matrix products, arithmetic and copies ran while one was open for 3% of the time, Pallas kernels for 0%

profile of v1, /device:TPU:1, one launch (start us, length us, event | category | flops | bytes accessed | tf_op | source)
XLA Modules:
  0.0 477.7 jit_solution(11799865904743419519)
XLA Ops:
  6.5 0.0 copy-start
  6.5 0.0 copy-start.6
  6.5 1.6 copy-done
  8.1 2.3 fusion.27
  10.4 1.6 copy.57
  12.0 5.9 %all-to-all-start.1 = ((f32[2,2,64,8,128]{4,3,1,0,2:T(8,128)}), f32[2,2,64,8,128]{4,3,1,0,2:T(8,128)}, u32[]{:S(2)}, u32[]{:S(2)}) async-start(f32[2,2,64,8,128]{4,3,1,0,2:T(8,128)} %copy.57), calls=%async_computation.1 | async-start | bytes 2097152 | tf_op jit(solution)/shard_map/all_to_all | solution.py:36
  17.9 0.0 copy-done.6
  17.9 3.5 fusion.23
  21.4 0.6 copy.51
  22.0 11.9 %all-to-all-done.1 = f32[2,2,64,8,128]{4,3,1,0,2:T(8,128)} async-done(((f32[2,2,64,8,128]{4,3,1,0,2:T(8,128)}), f32[2,2,64,8,128]{4,3,1,0,2:T(8,128)}, u32[]{:S(2)}, u32[]{:S(2)}) %all-to-all-start.1) | async-done | bytes 1048608 | tf_op jit(solution)/shard_map/all_to_all | solution.py:36
  33.8 7.9 %stack.12 = f32[16,2,8,64,1,256]{5,3,2,1,4,0:T(8,128)} broadcast(f32[2,8,64,256]{3,2,1,0:T(8,128)S(1)} %copy.51), dimensions={1,2,3,5} | broadcast | bytes 17825792 | tf_op jit(solution)/shard_map/stack | solution.py:11
  41.7 8.5 %all-to-all-start = ((f32[16,2,8,64,1,256]{5,3,2,1,4,0:T(8,128)}), f32[16,2,8,64,1,256]{5,3,2,1,4,0:T(8,128)}, u32[]{:S(2)}, u32[]{:S(2)}) async-start(f32[16,2,8,64,1,256]{5,3,2,1,4,0:T(8,128)} %stack.12), calls=%async_computation | async-start | bytes 33554432 | tf_op jit(solution)/shard_map/all_to_all | solution.py:12
  50.1 0.0 reduce-scatter.2.cloned.1.call-start
  50.2 1.3 copy.58
  51.5 0.1 fusion.37
  51.6 0.0 copy-start.7
  51.6 3.1 copy.65
  54.8 3.2 copy.61
  58.1 177.8 %all-to-all-done = f32[16,2,8,64,1,256]{5,3,2,1,4,0:T(8,128)} async-done(((f32[16,2,8,64,1,256]{5,3,2,1,4,0:T(8,128)}), f32[16,2,8,64,1,256]{5,3,2,1,4,0:T(8,128)}, u32[]{:S(2)}, u32[]{:S(2)}) %all-to-all-start) | async-done | bytes 16777248 | tf_op jit(solution)/shard_map/all_to_all | solution.py:12
  235.9 0.0 copy-done.7
  235.9 25.9 %fusion.20 = f32[2,8,64,8,256]{4,3,2,1,0:T(8,128)} fusion(f32[16,2,8,64,1,256]{5,3,2,1,4,0:T(8,128)} %all-to-all-done, f32[8,16]{1,0:T(8,128)S(1)} %copy-done.7), kind=kOutput, calls=%fused_computation.17 | convolution fusion | flops 402653184 | bytes 25166336 | tf_op jit(solution)/shard_map/cpqsm,ks->cpqkm/dot_general | solution.py:29
  261.8 0.0 copy-start.8
  261.8 12.2 %copy.53 = f32[2,8,64,8,256]{2,4,3,1,0:T(8,128)} copy(f32[2,8,64,8,256]{4,3,2,1,0:T(8,128)} %fusion.20) | data formatting | bytes 16777216 | tf_op jit(solution)/shard_map/cpqsm,ks->cpqkm/transpose | solution.py:29
  274.0 0.0 copy-done.8
  274.0 17.9 %fusion.17 = f32[2,8,64,8,8,16]{2,4,5,3,1,0:T(8,128)S(1)} fusion(f32[2,8,64,8,16,16]{2,5,4,3,1,0:T(8,128)} %bitcast.66, f32[8,16]{1,0:T(8,128)S(1)} %copy-done.8), kind=kOutput, calls=%fused_computation.16 | convolution fusion | flops 201326592 | bytes 12583424 | tf_op jit(solution)/shard_map/cpqktz,yt->cpqkyz/dot_general | solution.py:33
  291.9 1.1 fusion.36
  293.0 0.9 copy.62
  294.0 0.0 copy-start.2
  294.0 0.9 copy.55
  294.9 1.2 copy-done.2
  296.2 0.0 copy-start.3
  296.2 14.6 %fusion.7 = f32[8,128,64,16]{2,3,1,0:T(8,128)S(1)} fusion(f32[16,8,8,128]{0,1,3,2:T(8,128)S(1)} %copy-done.2, f32[8,64,8,128]{1,3,2,0:T(8,128)S(1)} %bitcast.67), kind=kOutput, calls=%fused_computation.10 | convolution fusion | flops 100663296 | bytes 6815744 | tf_op jit(solution)/shard_map/brkm,rqkm->bqkm/dot_general | solution.py:39
  310.8 0.0 copy-done.3
  310.8 14.3 %fusion.5 = f32[8,128,64,16]{2,3,1,0:T(8,128)S(1)} fusion(f32[16,8,8,128]{0,1,3,2:T(8,128)S(1)} %copy-done.3, f32[8,64,8,128]{1,3,2,0:T(8,128)S(1)} %bitcast.68), kind=kOutput, calls=%fused_computation.8 | convolution fusion | flops 100663296 | bytes 6815744 | tf_op jit(solution)/shard_map/brkm,rqkm->bqkm/dot_general | solution.py:40
  325.1 16.3 %subtract_bitcast_fusion = f32[1,16,64,8,128]{2,1,4,3,0:T(8,128)} fusion(f32[8,128,64,16]{2,3,1,0:T(8,128)S(1)} %fusion.7, f32[16,8,8,128]{0,1,3,2:T(8,128)S(1)} %copy-done.3, f32[8,64,8,128]{1,3,2,0:T(8,128)S(1)} %bitcast.64), kind=kOutput, calls=%fused_computation.7 | convolution fusion | flops 101711872 | bytes 11010048 | tf_op jit(solution)/shard_map/brkm,rqkm->bqkm/dot_general | solution.py:37
  341.4 0.0 copy-start.4
  341.4 14.4 %add_bitcast_fusion = f32[1,16,64,8,128]{2,1,4,3,0:T(8,128)S(1)} fusion(f32[8,128,64,16]{2,3,1,0:T(8,128)S(1)} %fusion.5, f32[16,8,8,128]{0,1,3,2:T(8,128)S(1)} %copy-done.2, f32[8,64,8,128]{1,3,2,0:T(8,128)S(1)} %bitcast.65), kind=kOutput, calls=%fused_computation.6 | convolution fusion | flops 101711872 | bytes 11010048 | tf_op jit(solution)/shard_map/brkm,rqkm->bqkm/dot_general | solution.py:42
  355.8 0.0 copy-done.4
  355.8 6.1 %pad_maximum_fusion = f32[2,16,64,8,128]{2,1,4,3,0:T(8,128)} fusion(f32[1,16,64,8,128]{2,1,4,3,0:T(8,128)S(1)} %add_bitcast_fusion, f32[1,16,64,8,128]{2,1,4,3,0:T(8,128)S(1)} %copy-done.4), kind=kLoop, calls=%fused_computation | loop fusion | flops 2097152 | bytes 16777216 | tf_op jit(solution)/shard_map/stack | solution.py:43
  362.0 11.1 %copy.70 = f32[2,16,64,8,128]{4,3,2,0,1:T(8,128)} copy(f32[2,16,64,8,128]{2,1,4,3,0:T(8,128)} %pad_maximum_fusion) | data formatting | bytes 16777216 | tf_op jit(solution)/shard_map/stack | solution.py:43
  373.0 0.0 copy-start.5
  373.0 0.0 reduce-scatter.2.cloned.1.call-update
  373.1 0.0 copy-start.1
  373.1 88.4 %reduce-scatter.2.cloned.1.call-done = f32[2,2,64,8,128]{4,3,2,0,1:T(8,128)} async-done(((f32[2,16,64,8,128]{4,3,2,0,1:T(8,128)}), f32[2,2,64,8,128]{4,3,2,0,1:T(8,128)}) %reduce-scatter.2.cloned.1.call-update) | async-done | bytes 1048592 | tf_op jit(solution)/shard_map/reduce_scatter | solution.py:44
  461.5 0.0 copy-done.5
  461.5 6.0 %convolution_bitcast_fusion = f32[2,2,128,8,128]{2,4,3,1,0:T(8,128)} fusion(f32[2,2,64,8,128]{4,3,2,0,1:T(8,128)} %reduce-scatter.2.cloned.1.call-done, f32[128,64]{0,1:T(8,128)S(1)} %copy-done.5), kind=kOutput, calls=%fused_computation.22 | convolution fusion | flops 402653184 | bytes 3178496 | tf_op jit(solution)/shard_map/oq,cbqkm->cbokm/dot_general | solution.py:45
  467.5 2.9 copy.72
  470.4 0.0 copy-done.1
  (2 shorter events, 0.1 us)
Async XLA Ops:
  6.5 1.6 copy-start
  6.5 11.3 %copy-start.6 = (f32[16,16]{1,0:T(8,128)S(1)}, f32[16,16]{1,0:T(8,128)}, u32[]{:S(2)}) copy-start(f32[16,16]{1,0:T(8,128)} %param.13) | copy-start | bytes 3076
  12.0 21.8 %all-to-all-start.1 = ((f32[2,2,64,8,128]{4,3,1,0,2:T(8,128)}), f32[2,2,64,8,128]{4,3,1,0,2:T(8,128)}, u32[]{:S(2)}, u32[]{:S(2)}) async-start(f32[2,2,64,8,128]{4,3,1,0,2:T(8,128)} %copy.57), calls=%async_computation.1 | async-start | bytes 2097152 | tf_op jit(solution)/shard_map/all_to_all | solution.py:36
  41.7 194.2 %all-to-all-start = ((f32[16,2,8,64,1,256]{5,3,2,1,4,0:T(8,128)}), f32[16,2,8,64,1,256]{5,3,2,1,4,0:T(8,128)}, u32[]{:S(2)}, u32[]{:S(2)}) async-start(f32[16,2,8,64,1,256]{5,3,2,1,4,0:T(8,128)} %stack.12), calls=%async_computation | async-start | bytes 33554432 | tf_op jit(solution)/shard_map/all_to_all | solution.py:12
  50.1 411.3 %reduce-scatter.2.cloned.1.call-start = ((), (), s32[]{:S(2)}) async-start(), calls=%async_computation.3 | async-start | bytes 9437184 | tf_op jit(solution)/shard_map/reduce_scatter | solution.py:44
  51.6 184.2 %copy-start.7 = (f32[8,16]{1,0:T(8,128)S(1)}, f32[8,16]{1,0:T(8,128)}, u32[]{:S(2)}) copy-start(f32[8,16]{1,0:T(8,128)} %param.11) | copy-start | bytes 1540
  261.8 12.2 %copy-start.8 = (f32[8,16]{1,0:T(8,128)S(1)}, f32[8,16]{1,0:T(8,128)}, u32[]{:S(2)}) copy-start(f32[8,16]{1,0:T(8,128)} %param.12) | copy-start | bytes 1540
  294.0 2.2 copy-start.2
  296.2 14.6 %copy-start.3 = (f32[16,8,8,128]{0,1,3,2:T(8,128)S(1)}, f32[16,8,8,128]{0,1,3,2:T(8,128)}, u32[]{:S(2)}) copy-start(f32[16,8,8,128]{0,1,3,2:T(8,128)} %copy.61) | copy-start | bytes 1572868
  341.4 14.4 %copy-start.4 = (f32[1,16,64,8,128]{2,1,4,3,0:T(8,128)S(1)}, f32[1,16,64,8,128]{2,1,4,3,0:T(8,128)}, u32[]{:S(2)}) copy-start(f32[1,16,64,8,128]{2,1,4,3,0:T(8,128)} %subtract_bitcast_fusion) | copy-start | bytes 12582916
  373.0 88.5 %copy-start.5 = (f32[128,64]{0,1:T(8,128)S(1)}, f32[128,64]{0,1:T(8,128)}, u32[]{:S(2)}) copy-start(f32[128,64]{0,1:T(8,128)} %param.10) | copy-start | bytes 98308
  373.1 97.3 %copy-start.1 = (f32[2,2,128,8,128]{4,3,2,1,0:T(8,128)S(1)}, f32[2,2,128,8,128]{4,3,2,1,0:T(8,128)}, u32[]{:S(2)}) copy-start(f32[2,2,128,8,128]{4,3,2,1,0:T(8,128)} %param.7) | copy-start | bytes 6291460
Sparse Core Ops, SparseCore 0:
  373.2 88.2 reduce-scatter.1
